TPU v7x, 512 devices: a whole 4x8x8 slice. The times are simulated.
512 devices in a mesh: gx: 32 (over z, x_hi, core), gy: 16 (over y, x_lo).
Axes of the slice: x: 4 (x_hi: 2, x_lo: 2; x = x_hi * 2 + x_lo), y: 8, z: 8, core: 2. Of those that a mesh axis runs over, the one named last changes fastest.
Arguments:
- init_re: float32 [1, 1024, 16384], P(None, 'gx', 'gy'), may hold values from -6 to 6
- init_im: float32 [1, 1024, 16384], P(None, 'gx', 'gy'), may hold values from -6 to 6
- onsite: float32 [1024, 16384], P('gx', 'gy'), may hold values from -0.9 to 0.9
- bond_x: int32 [1024, 16384], P('gx', 'gy'), may hold values from 0 to 15
- bond_y: int32 [1024, 16384], P('gx', 'gy'), may hold values from 0 to 15
- hop_table: float32 [16], replicated, may hold values from 1.4 to 1.6
- centre: int32 [1, 2], replicated, may hold values from 0 to 1023
- duration: float32 [1], replicated, may hold values from 0.55 to 0.6
Outputs:
- out_re: float32 [1, 1024, 16384], P(None, 'gx', 'gy')
- out_im: float32 [1, 1024, 16384], P(None, 'gx', 'gy')
- term_norms: float32 [2, 8, 1], replicated
All inputs are finite; a program needn't handle non-finite values.
Results may differ from a plain program's by a relative error of at most 0.0003.
Values sent between devices are 32-bit elements; how exact they have to be, the bound alone decides.
No kernel may reach another device: no remote copies, remote signals or barrier semaphores. Data moves between devices by JAX's collectives and lax.ppermute only.
A program may use at most 64 MiB of HBM per device.

v0:
```python
import math
import jax
import jax.numpy as jnp
from jax import lax
from jax.sharding import Mesh
from jax.sharding import PartitionSpec as P

TERMS = 8
STEPS = 2
GX = ("gx_0", "gx_1", "gx_2")
GY = ("gy_0", "gy_1")
GX_GY = ("gx_0", "gx_1", "gx_2", "gy_0", "gy_1")
SPECTRAL = 7.5
epsilon = 1e-06


def padded(block, sides, width):
    for axis, dim in sides:
        count = lax.axis_size(axis)
        forward = [(i, i + 1) for i in range(count - 1)]
        forward.append((count - 1, 0))
        backward = [(target, source) for source, target in forward]
        low = lax.ppermute(
            lax.slice_in_dim(block, block.shape[dim] - width, None, axis=dim), axis, forward
        )
        high = lax.ppermute(lax.slice_in_dim(block, 0, width, axis=dim), axis, backward)
        block = jnp.concatenate([low, block, high], axis=dim)
    return block


def over_axes(value, axes):
    for axis in axes:
        value = lax.psum(value, axis)
    return value


def bessel_weights(duration):
    argument = duration[0] * SPECTRAL
    halved = argument * 0.5
    weights = []
    for degree in range(TERMS):
        series = halved**degree / math.factorial(degree)
        summed = series
        for counter in range(1, 24):
            series = series * -(halved * halved) / (counter * (counter + degree))
            summed = summed + series
        weights.append(summed if degree == 0 else 2.0 * summed)
    return weights


def rotated(degree, real_part, imag_part):
    quarter = degree % 4
    if quarter == 0:
        return (real_part, imag_part)
    if quarter == 1:
        return (imag_part, -real_part)
    if quarter == 2:
        return (-real_part, -imag_part)
    return (-imag_part, real_part)


def falloff(positions, centres, extent):
    distance = jnp.mod(positions[None, :] - centres[:, None], extent)
    distance = jnp.minimum(distance, extent - distance).astype(jnp.float32)
    return distance * distance * (4.5 / (extent * extent))


def shrink(tensor, margin):
    if margin == 0:
        return tensor
    return tensor[..., margin : tensor.shape[-2] - margin, margin : tensor.shape[-1] - margin]


def apply_wide(grid_field, coeffs):
    potential = coeffs[0]
    hop_rows = coeffs[1]
    hop_cols = coeffs[2]
    result = potential[1:-1, 1:-1] * grid_field[..., 1:-1, 1:-1]
    result = result - hop_rows[1:-1, 1:-1] * grid_field[..., 2:, 1:-1]
    result = result - hop_rows[:-2, 1:-1] * grid_field[..., :-2, 1:-1]
    result = result - hop_cols[1:-1, 1:-1] * grid_field[..., 1:-1, 2:]
    result = result - hop_cols[1:-1, :-2] * grid_field[..., 1:-1, :-2]
    return result * (1.0 / SPECTRAL)


def per_device(init_re, init_im, onsite, bond_x, bond_y, hop_table, centre, duration):
    packets, rows_local, cols_local = init_re.shape
    rows_total = rows_local * lax.axis_size(GX)
    cols_total = cols_local * lax.axis_size(GY)
    cell_count = rows_total * cols_total
    classes = hop_table.shape[0]
    selector = jnp.arange(classes, dtype=jnp.int32)[:, None, None]
    table_column = hop_table[:, None, None]
    hop_down = jnp.sum(jnp.where(bond_x[None] == selector, table_column, 0.0), axis=0)
    hop_right = jnp.sum(jnp.where(bond_y[None] == selector, table_column, 0.0), axis=0)
    weights = bessel_weights(duration)
    row_index = lax.axis_index(GX) * rows_local + lax.iota(jnp.int32, rows_local)
    col_index = lax.axis_index(GY) * cols_local + lax.iota(jnp.int32, cols_local)
    row_fall = falloff(row_index, centre[:, 0], rows_total)
    col_fall = falloff(col_index, centre[:, 1], cols_total)
    envelope = jnp.exp(-(row_fall[:, :, None] + col_fall[:, None, :]))
    packet_state = jnp.stack([init_re * envelope, init_im * envelope])
    reach = TERMS - 1
    coeffs = padded(jnp.stack([onsite, hop_down, hop_right]), ((GX, 1), (GY, 2)), reach)
    norm_rows = []
    local_terms = []
    local_states = []
    for repeat in range(STEPS):
        current = padded(packet_state, ((GX, 2), (GY, 3)), reach)
        margin = reach
        previous = current
        previous_margin = reach
        chebyshev = [packet_state]
        for chebyshev_degree in range(1, TERMS):
            applied = apply_wide(current, shrink(coeffs, reach - margin))
            if chebyshev_degree == 1:
                following = applied
            else:
                following = 2.0 * applied - shrink(previous, previous_margin - margin + 1)
            previous, previous_margin = (current, margin)
            current = following
            margin = margin - 1
            chebyshev.append(shrink(following, margin))
        accumulate = weights[0] * packet_state
        for degree in range(1, TERMS):
            real_rot, imag_rot = rotated(degree, chebyshev[degree][0], chebyshev[degree][1])
            accumulate = accumulate + weights[degree] * jnp.stack([real_rot, imag_rot])
        term_local = jnp.stack([jnp.sum(vector * vector, axis=(0, 2, 3)) for vector in chebyshev])
        state_local = jnp.sum(accumulate * accumulate, axis=(0, 2, 3))
        local_terms.append(term_local)
        local_states.append(state_local)
        packet_state = accumulate
    term_totals, state_totals = (
        over_axes(jnp.stack(local_terms), GX_GY),
        over_axes(jnp.stack(local_states), GX_GY),
    )
    factor = jnp.ones((packets,), jnp.float32)
    for repeat in range(STEPS):
        squared = factor * factor
        norm_rows.append(term_totals[repeat] / cell_count * squared)
        true_mean = state_totals[repeat] / cell_count * squared
        factor = factor * lax.rsqrt(true_mean + epsilon)
    packet_state = packet_state * factor[None, :, None, None]
    return (packet_state[0], packet_state[1], jnp.stack(norm_rows))


def solution(mesh):
    finer = Mesh(mesh.devices.reshape(8, 2, 2, 8, 2), ("gx_0", "gx_1", "gx_2", "gy_0", "gy_1"))
    in_specs = (P(None, GX, GY), P(None, GX, GY), P(GX, GY), P(GX, GY), P(GX, GY), P(), P(), P())
    out_specs = (P(None, GX, GY), P(None, GX, GY), P())
    return jax.shard_map(
        per_device, mesh=finer, in_specs=in_specs, out_specs=out_specs, check_vma=False
    )
```

profile of v0, /device:TPU:2, one launch (start us, length us, event | category | flops | bytes accessed | tf_op | source)
XLA Modules:
  0.0 154.3 jit_solution(2345416832036996871)
XLA Ops:
  0.7 1.3 fusion.129
  2.0 0.7 fusion.100
  2.6 0.7 fusion.97
  3.3 1.1 multiply_bitcast_fusion
  4.4 1.9 %collective-permute-start.4 = (f32[2,1,7,1024]{3,2,1,0:T(8,128)S(1)}, f32[2,1,7,1024]{3,2,1,0:T(8,128)S(1)}, u32[]{:S(2)}, u32[]{:S(2)}) collective-permute-start(f32[2,1,7,1024]{3,2,1,0:T(8,128)S(1)} %get-tuple-element.84), channel_id=1, source_target_pairs={{0,16},{16,32},{32,48},{48,64},{64,80},{80,96},{96,112},{112,128},... | collective-permute-start | bytes 172040 | tf_op jit(solution)/shard_map/ppermute | solution.py:23
  6.4 11.9 %collective-permute-start.5 = (f32[2,1,7,1024]{3,2,1,0:T(8,128)S(1)}, f32[2,1,7,1024]{3,2,1,0:T(8,128)S(1)}, u32[]{:S(2)}, u32[]{:S(2)}) collective-permute-start(f32[2,1,7,1024]{3,2,1,0:T(8,128)S(1)} %get-tuple-element.85), channel_id=1, source_target_pairs={{16,0},{32,16},{48,32},{64,48},{80,64},{96,80},{112,96},{128,112},... | collective-permute-start | bytes 172040 | tf_op jit(solution)/shard_map/ppermute | solution.py:26
  18.9 1.9 %collective-permute-start = (f32[3,7,1024]{2,1,0:T(8,128)S(1)}, f32[3,7,1024]{2,1,0:T(8,128)S(1)}, u32[]{:S(2)}, u32[]{:S(2)}) collective-permute-start(f32[3,7,1024]{2,1,0:T(8,128)S(1)} %get-tuple-element.56), channel_id=1, source_target_pairs={{0,16},{16,32},{32,48},{48,64},{64,80},{80,96},{96,112},{112,128},... | collective-permute-start | bytes 258056 | tf_op jit(solution)/shard_map/ppermute | solution.py:23
  20.8 7.3 %collective-permute-start.1 = (f32[3,7,1024]{2,1,0:T(8,128)S(1)}, f32[3,7,1024]{2,1,0:T(8,128)S(1)}, u32[]{:S(2)}, u32[]{:S(2)}) collective-permute-start(f32[3,7,1024]{2,1,0:T(8,128)S(1)} %get-tuple-element.57), channel_id=1, source_target_pairs={{16,0},{32,16},{48,32},{64,48},{80,64},{96,80},{112,96},{128,112},... | collective-permute-start | bytes 258056 | tf_op jit(solution)/shard_map/ppermute | solution.py:26
  29.4 0.6 multiply_reduce_fusion.8
  30.4 3.3 %collective-permute-start.3 = (f32[3,46,7]{2,1,0:T(8,128)S(1)}, f32[3,46,7]{2,1,0:T(8,128)S(1)}, u32[]{:S(2)}, u32[]{:S(2)}) collective-permute-start(f32[3,46,7]{2,1,0:T(8,128)S(1)} %get-tuple-element.44), channel_id=1, source_target_pairs={{1,0},{2,1},{3,2},{4,3},{5,4},{6,5},{7,6},{8,7},{9,8},{10,9},{11,1... | collective-permute-start | bytes 11600 | tf_op jit(solution)/shard_map/ppermute | solution.py:26
  33.8 3.4 %collective-permute-start.2 = (f32[3,46,7]{2,1,0:T(8,128)S(1)}, f32[3,46,7]{2,1,0:T(8,128)S(1)}, u32[]{:S(2)}, u32[]{:S(2)}) collective-permute-start(f32[3,46,7]{2,1,0:T(8,128)S(1)} %get-tuple-element.45), channel_id=1, source_target_pairs={{0,1},{1,2},{2,3},{3,4},{4,5},{5,6},{6,7},{7,8},{8,9},{9,10},{10,1... | collective-permute-start | bytes 11600 | tf_op jit(solution)/shard_map/ppermute | solution.py:23
  37.3 3.9 %collective-permute-start.7 = (f32[2,1,46,7]{3,2,1,0:T(8,128)S(1)}, f32[2,1,46,7]{3,2,1,0:T(8,128)S(1)}, u32[]{:S(2)}, u32[]{:S(2)}) collective-permute-start(f32[2,1,46,7]{3,2,1,0:T(8,128)S(1)} %get-tuple-element.58), channel_id=1, source_target_pairs={{1,0},{2,1},{3,2},{4,3},{5,4},{6,5},{7,6},{8,7},{9,8},{10,9},{11,1... | collective-permute-start | bytes 7736 | tf_op jit(solution)/shard_map/ppermute | solution.py:26
  41.2 2.8 %collective-permute-start.6 = (f32[2,1,46,7]{3,2,1,0:T(8,128)S(1)}, f32[2,1,46,7]{3,2,1,0:T(8,128)S(1)}, u32[]{:S(2)}, u32[]{:S(2)}) collective-permute-start(f32[2,1,46,7]{3,2,1,0:T(8,128)S(1)} %get-tuple-element.59), channel_id=1, source_target_pairs={{0,1},{1,2},{2,3},{3,4},{4,5},{5,6},{6,7},{7,8},{8,9},{9,10},{10,1... | collective-permute-start | bytes 7736 | tf_op jit(solution)/shard_map/ppermute | solution.py:23
  44.1 5.1 %collective-permute-done.6 = f32[2,1,46,7]{3,2,1,0:T(8,128)S(1)} collective-permute-done((f32[2,1,46,7]{3,2,1,0:T(8,128)S(1)}, f32[2,1,46,7]{3,2,1,0:T(8,128)S(1)}, u32[]{:S(2)}, u32[]{:S(2)}) %collective-permute-start.6) | collective-permute-done | bytes 2608 | tf_op jit(solution)/shard_map/ppermute | solution.py:23
  52.2 0.8 fusion.65
  53.5 0.7 slice_subtract_fusion.1
  54.2 0.8 fusion.64
  60.7 1.1 multiply_reduce_fusion.4
  61.8 0.9 multiply_reduce_fusion.10
  62.8 1.9 %collective-permute-start.8 = (f32[2,1,7,1024]{3,2,1,0:T(8,128)S(1)}, f32[2,1,7,1024]{3,2,1,0:T(8,128)S(1)}, u32[]{:S(2)}, u32[]{:S(2)}) collective-permute-start(f32[2,1,7,1024]{3,2,1,0:T(8,128)S(1)} %get-tuple-element.80), channel_id=1, source_target_pairs={{0,16},{16,32},{32,48},{48,64},{64,80},{80,96},{96,112},{112,128},... | collective-permute-start | bytes 172040 | tf_op jit(solution)/shard_map/ppermute | solution.py:23
  64.7 7.3 %collective-permute-start.9 = (f32[2,1,7,1024]{3,2,1,0:T(8,128)S(1)}, f32[2,1,7,1024]{3,2,1,0:T(8,128)S(1)}, u32[]{:S(2)}, u32[]{:S(2)}) collective-permute-start(f32[2,1,7,1024]{3,2,1,0:T(8,128)S(1)} %get-tuple-element.81), channel_id=1, source_target_pairs={{16,0},{32,16},{48,32},{64,48},{80,64},{96,80},{112,96},{128,112},... | collective-permute-start | bytes 172040 | tf_op jit(solution)/shard_map/ppermute | solution.py:26
  72.0 0.8 fusion.63
  72.8 1.1 collective-permute-done.9
  74.0 6.0 %collective-permute-start.11 = (f32[2,1,46,7]{3,2,1,0:T(8,128)S(1)}, f32[2,1,46,7]{3,2,1,0:T(8,128)S(1)}, u32[]{:S(2)}, u32[]{:S(2)}) collective-permute-start(f32[2,1,46,7]{3,2,1,0:T(8,128)S(1)} %get-tuple-element.54), channel_id=1, source_target_pairs={{1,0},{2,1},{3,2},{4,3},{5,4},{6,5},{7,6},{8,7},{9,8},{10,9},{11,1... | collective-permute-start | bytes 7736 | tf_op jit(solution)/shard_map/ppermute | solution.py:26
  80.0 2.1 %collective-permute-start.10 = (f32[2,1,46,7]{3,2,1,0:T(8,128)S(1)}, f32[2,1,46,7]{3,2,1,0:T(8,128)S(1)}, u32[]{:S(2)}, u32[]{:S(2)}) collective-permute-start(f32[2,1,46,7]{3,2,1,0:T(8,128)S(1)} %get-tuple-element.55), channel_id=1, source_target_pairs={{0,1},{1,2},{2,3},{3,4},{4,5},{5,6},{6,7},{7,8},{8,9},{9,10},{10,1... | collective-permute-start | bytes 7736 | tf_op jit(solution)/shard_map/ppermute | solution.py:23
  82.2 0.8 multiply_reduce_fusion.7
  82.9 5.1 %stack.186 = f32[8,1]{0,1:T(1,128)S(1)} concatenate(f32[1,1]{0,1:T(1,128)} %bitcast.36, f32[1,1]{0,1:T(1,128)} %bitcast.37, f32[1,1]{0,1:T(1,128)} %bitcast.38, f32[1,1]{0,1:T(1,128)} %bitcast.39, f32[1,1]{0,1:T(1,128)} %bitcast.40, f32[1,1]{0,1:T(1,128)} %bitcast.41, f32[1,1]{0,1:T(1,128)} %bitcast.42, f32[1,1]{0,1:T(1,128)} %bitcast.43), dimensions={0} | concatenate | bytes 64 | tf_op jit(solution)/shard_map/stack | solution.py:128
  88.8 0.7 fusion.62
  89.6 0.7 slice_subtract_fusion
  90.2 0.8 fusion.61
  91.1 0.6 slice_subtract_fusion.5
  91.7 0.7 fusion.60
  92.5 0.6 slice_subtract_fusion.4
  93.0 0.8 multiply_reduce_fusion.3
  94.7 0.6 copy-done.25
  95.6 0.6 slice_subtract_fusion.2
  96.8 1.0 multiply_reduce_fusion
  98.2 5.1 %stack.195 = f32[8,1]{0,1:T(1,128)S(1)} concatenate(f32[1,1]{0,1:T(1,128)} %bitcast.29, f32[1,1]{0,1:T(1,128)} %bitcast.45, f32[1,1]{0,1:T(1,128)} %bitcast.46, f32[1,1]{0,1:T(1,128)} %bitcast.47, f32[1,1]{0,1:T(1,128)} %bitcast.48, f32[1,1]{0,1:T(1,128)} %bitcast.49, f32[1,1]{0,1:T(1,128)} %bitcast.50, f32[1,1]{0,1:T(1,128)} %bitcast.51), dimensions={0} | concatenate | bytes 64 | tf_op jit(solution)/shard_map/stack | solution.py:128
  103.4 0.8 multiply_reduce_fusion.9
  104.2 1.4 pad_maximum_fusion.9
  105.6 14.8 %all-reduce.1 = (f32[2,1]{0,1:T(1,128)S(1)}, f32[2,8,1]{1,2,0:T(1,128)S(1)}) all-reduce(f32[2,1]{0,1:T(1,128)S(1)} %pad_maximum_fusion.9, f32[2,8,1]{1,2,0:T(1,128)S(1)} %pad_maximum_fusion.7), channel_id=1, replica_groups=mesh['gx_0'=8,'gx_1'=2,'gx_2'=2,'gy_0'=8,'gy_1'=2] {'gx_0'}, use_global_device_ids=true, to_apply=%region_4.5 | all-reduce | flops 18 | bytes 144 | tf_op jit(solution)/shard_map/psum | solution.py:33
  120.5 6.4 %all-reduce.4 = (f32[2,1]{0,1:T(1,128)S(1)}, f32[2,8,1]{1,2,0:T(1,128)S(1)}) all-reduce(f32[2,1]{0,1:T(1,128)S(1)} %get-tuple-element.7, f32[2,8,1]{1,2,0:T(1,128)S(1)} %get-tuple-element.8), channel_id=1, replica_groups=mesh['gx_0'=8,'gx_1'=2,'gx_2'=2,'gy_0'=8,'gy_1'=2] {'gx_1'}, use_global_device_ids=true, to_apply=%region_5.6 | all-reduce | flops 18 | bytes 144 | tf_op jit(solution)/shard_map/psum | solution.py:33
  126.9 2.4 %all-reduce.3 = (f32[2,1]{0,1:T(1,128)S(1)}, f32[2,8,1]{1,2,0:T(1,128)S(1)}) all-reduce(f32[2,1]{0,1:T(1,128)S(1)} %get-tuple-element.13, f32[2,8,1]{1,2,0:T(1,128)S(1)} %get-tuple-element.14), channel_id=1, replica_groups=mesh['gx_0'=8,'gx_1'=2,'gx_2'=2,'gy_0'=8,'gy_1'=2] {'gx_2'}, use_global_device_ids=true, to_apply=%region_6.7 | all-reduce | flops 18 | bytes 144 | tf_op jit(solution)/shard_map/psum | solution.py:33
  129.3 16.8 %all-reduce = (f32[2,1]{0,1:T(1,128)S(1)}, f32[2,8,1]{1,2,0:T(1,128)S(1)}) all-reduce(f32[2,1]{0,1:T(1,128)S(1)} %get-tuple-element.11, f32[2,8,1]{1,2,0:T(1,128)S(1)} %get-tuple-element.12), channel_id=1, replica_groups=mesh['gx_0'=8,'gx_1'=2,'gx_2'=2,'gy_0'=8,'gy_1'=2] {'gy_0'}, use_global_device_ids=true, to_apply=%region_7.8 | all-reduce | flops 18 | bytes 144 | tf_op jit(solution)/shard_map/psum | solution.py:33
  146.1 4.9 %all-reduce.2 = (f32[2,1]{0,1:T(1,128)S(1)}, f32[2,8,1]{1,2,0:T(1,128)S(1)}) all-reduce(f32[2,1]{0,1:T(1,128)S(1)} %get-tuple-element.5, f32[2,8,1]{1,2,0:T(1,128)S(1)} %get-tuple-element.6), channel_id=1, replica_groups=mesh['gx_0'=8,'gx_1'=2,'gx_2'=2,'gy_0'=8,'gy_1'=2] {'gy_1'}, use_global_device_ids=true, to_apply=%region_8.9 | all-reduce | flops 18 | bytes 144 | tf_op jit(solution)/shard_map/psum | solution.py:33
  151.0 0.6 fusion.128
  153.0 0.7 slice_bitcast_fusion.21
  153.8 0.6 pad_maximum_fusion.8
  (173 shorter events, 12.9 us)
Async XLA Ops:
  0.6 17.7 %copy-start.53 = (f32[16]{0:T(128)S(1)}, f32[16]{0:T(128)}, u32[]{:S(2)}) copy-start(f32[16]{0:T(128)} %param.13) | copy-start | bytes 196
  0.6 17.7 %copy-start.52 = (s32[32,1024]{1,0:T(8,128)S(1)}, s32[32,1024]{1,0:T(8,128)}, u32[]{:S(2)}) copy-start(s32[32,1024]{1,0:T(8,128)} %param.12) | copy-start | bytes 393220
  0.7 17.7 %copy-start.51 = (s32[32,1024]{1,0:T(8,128)S(1)}, s32[32,1024]{1,0:T(8,128)}, u32[]{:S(2)}) copy-start(s32[32,1024]{1,0:T(8,128)} %param.11) | copy-start | bytes 393220
  3.3 15.5 %copy-start.50 = (f32[32,1024]{1,0:T(8,128)S(1)}, f32[32,1024]{1,0:T(8,128)}, u32[]{:S(2)}) copy-start(f32[32,1024]{1,0:T(8,128)} %param.10) | copy-start | bytes 393220
  4.4 25.6 %collective-permute-start.4 = (f32[2,1,7,1024]{3,2,1,0:T(8,128)S(1)}, f32[2,1,7,1024]{3,2,1,0:T(8,128)S(1)}, u32[]{:S(2)}, u32[]{:S(2)}) collective-permute-start(f32[2,1,7,1024]{3,2,1,0:T(8,128)S(1)} %get-tuple-element.84), channel_id=1, source_target_pairs={{0,16},{16,32},{32,48},{48,64},{64,80},{80,96},{96,112},{112,128},... | collective-permute-start | bytes 172040 | tf_op jit(solution)/shard_map/ppermute | solution.py:23
  6.4 23.6 %collective-permute-start.5 = (f32[2,1,7,1024]{3,2,1,0:T(8,128)S(1)}, f32[2,1,7,1024]{3,2,1,0:T(8,128)S(1)}, u32[]{:S(2)}, u32[]{:S(2)}) collective-permute-start(f32[2,1,7,1024]{3,2,1,0:T(8,128)S(1)} %get-tuple-element.85), channel_id=1, source_target_pairs={{16,0},{32,16},{48,32},{64,48},{80,64},{96,80},{112,96},{128,112},... | collective-permute-start | bytes 172040 | tf_op jit(solution)/shard_map/ppermute | solution.py:26
  18.9 11.2 %collective-permute-start = (f32[3,7,1024]{2,1,0:T(8,128)S(1)}, f32[3,7,1024]{2,1,0:T(8,128)S(1)}, u32[]{:S(2)}, u32[]{:S(2)}) collective-permute-start(f32[3,7,1024]{2,1,0:T(8,128)S(1)} %get-tuple-element.56), channel_id=1, source_target_pairs={{0,16},{16,32},{32,48},{48,64},{64,80},{80,96},{96,112},{112,128},... | collective-permute-start | bytes 258056 | tf_op jit(solution)/shard_map/ppermute | solution.py:23
  20.8 9.5 %collective-permute-start.1 = (f32[3,7,1024]{2,1,0:T(8,128)S(1)}, f32[3,7,1024]{2,1,0:T(8,128)S(1)}, u32[]{:S(2)}, u32[]{:S(2)}) collective-permute-start(f32[3,7,1024]{2,1,0:T(8,128)S(1)} %get-tuple-element.57), channel_id=1, source_target_pairs={{16,0},{32,16},{48,32},{64,48},{80,64},{96,80},{112,96},{128,112},... | collective-permute-start | bytes 258056 | tf_op jit(solution)/shard_map/ppermute | solution.py:26
  30.4 19.1 %collective-permute-start.3 = (f32[3,46,7]{2,1,0:T(8,128)S(1)}, f32[3,46,7]{2,1,0:T(8,128)S(1)}, u32[]{:S(2)}, u32[]{:S(2)}) collective-permute-start(f32[3,46,7]{2,1,0:T(8,128)S(1)} %get-tuple-element.44), channel_id=1, source_target_pairs={{1,0},{2,1},{3,2},{4,3},{5,4},{6,5},{7,6},{8,7},{9,8},{10,9},{11,1... | collective-permute-start | bytes 11600 | tf_op jit(solution)/shard_map/ppermute | solution.py:26
  33.8 15.8 %collective-permute-start.2 = (f32[3,46,7]{2,1,0:T(8,128)S(1)}, f32[3,46,7]{2,1,0:T(8,128)S(1)}, u32[]{:S(2)}, u32[]{:S(2)}) collective-permute-start(f32[3,46,7]{2,1,0:T(8,128)S(1)} %get-tuple-element.45), channel_id=1, source_target_pairs={{0,1},{1,2},{2,3},{3,4},{4,5},{5,6},{6,7},{7,8},{8,9},{9,10},{10,1... | collective-permute-start | bytes 11600 | tf_op jit(solution)/shard_map/ppermute | solution.py:23
  37.3 6.9 %collective-permute-start.7 = (f32[2,1,46,7]{3,2,1,0:T(8,128)S(1)}, f32[2,1,46,7]{3,2,1,0:T(8,128)S(1)}, u32[]{:S(2)}, u32[]{:S(2)}) collective-permute-start(f32[2,1,46,7]{3,2,1,0:T(8,128)S(1)} %get-tuple-element.58), channel_id=1, source_target_pairs={{1,0},{2,1},{3,2},{4,3},{5,4},{6,5},{7,6},{8,7},{9,8},{10,9},{11,1... | collective-permute-start | bytes 7736 | tf_op jit(solution)/shard_map/ppermute | solution.py:26
  41.2 8.1 %collective-permute-start.6 = (f32[2,1,46,7]{3,2,1,0:T(8,128)S(1)}, f32[2,1,46,7]{3,2,1,0:T(8,128)S(1)}, u32[]{:S(2)}, u32[]{:S(2)}) collective-permute-start(f32[2,1,46,7]{3,2,1,0:T(8,128)S(1)} %get-tuple-element.59), channel_id=1, source_target_pairs={{0,1},{1,2},{2,3},{3,4},{4,5},{5,6},{6,7},{7,8},{8,9},{9,10},{10,1... | collective-permute-start | bytes 7736 | tf_op jit(solution)/shard_map/ppermute | solution.py:23
  55.4 2.3 %copy-start.4 = (f32[38,1030]{1,0:T(8,128)}, f32[38,1030]{1,0:T(8,128)S(1)}, u32[]{:S(2)}) copy-start(f32[38,1030]{1,0:T(8,128)S(1)} %slice.930) | copy-start | bytes 469684
  55.5 3.0 %copy-start.2 = (f32[36,1028]{1,0:T(8,128)}, f32[36,1028]{1,0:T(8,128)S(1)}, u32[]{:S(2)}) copy-start(f32[36,1028]{1,0:T(8,128)S(1)} %slice.944) | copy-start | bytes 444100
  55.6 5.1 %copy-start.40 = (f32[32,1024]{1,0:T(8,128)}, f32[32,1024]{1,0:T(8,128)S(1)}, u32[]{:S(2)}) copy-start(f32[32,1024]{1,0:T(8,128)S(1)} %slice.976) | copy-start | bytes 393220
  57.4 1.2 copy-start.16
  57.4 1.2 copy-start.18
  57.4 1.1 copy-start.20
  57.4 1.1 copy-start.22
  60.6 1.2 copy-start.42
  60.7 1.1 copy-start.44
  60.7 1.1 copy-start.46
  60.7 1.1 copy-start.48
  62.8 10.0 %collective-permute-start.8 = (f32[2,1,7,1024]{3,2,1,0:T(8,128)S(1)}, f32[2,1,7,1024]{3,2,1,0:T(8,128)S(1)}, u32[]{:S(2)}, u32[]{:S(2)}) collective-permute-start(f32[2,1,7,1024]{3,2,1,0:T(8,128)S(1)} %get-tuple-element.80), channel_id=1, source_target_pairs={{0,16},{16,32},{32,48},{48,64},{64,80},{80,96},{96,112},{112,128},... | collective-permute-start | bytes 172040 | tf_op jit(solution)/shard_map/ppermute | solution.py:23
  64.7 9.1 %collective-permute-start.9 = (f32[2,1,7,1024]{3,2,1,0:T(8,128)S(1)}, f32[2,1,7,1024]{3,2,1,0:T(8,128)S(1)}, u32[]{:S(2)}, u32[]{:S(2)}) collective-permute-start(f32[2,1,7,1024]{3,2,1,0:T(8,128)S(1)} %get-tuple-element.81), channel_id=1, source_target_pairs={{16,0},{32,16},{48,32},{64,48},{80,64},{96,80},{112,96},{128,112},... | collective-permute-start | bytes 172040 | tf_op jit(solution)/shard_map/ppermute | solution.py:26
  74.0 14.0 %collective-permute-start.11 = (f32[2,1,46,7]{3,2,1,0:T(8,128)S(1)}, f32[2,1,46,7]{3,2,1,0:T(8,128)S(1)}, u32[]{:S(2)}, u32[]{:S(2)}) collective-permute-start(f32[2,1,46,7]{3,2,1,0:T(8,128)S(1)} %get-tuple-element.54), channel_id=1, source_target_pairs={{1,0},{2,1},{3,2},{4,3},{5,4},{6,5},{7,6},{8,7},{9,8},{10,9},{11,1... | collective-permute-start | bytes 7736 | tf_op jit(solution)/shard_map/ppermute | solution.py:26
  80.0 8.0 %collective-permute-start.10 = (f32[2,1,46,7]{3,2,1,0:T(8,128)S(1)}, f32[2,1,46,7]{3,2,1,0:T(8,128)S(1)}, u32[]{:S(2)}, u32[]{:S(2)}) collective-permute-start(f32[2,1,46,7]{3,2,1,0:T(8,128)S(1)} %get-tuple-element.55), channel_id=1, source_target_pairs={{0,1},{1,2},{2,3},{3,4},{4,5},{5,6},{6,7},{7,8},{8,9},{9,10},{10,1... | collective-permute-start | bytes 7736 | tf_op jit(solution)/shard_map/ppermute | solution.py:23
  88.3 1.3 copy-start.1
  89.6 1.5 copy-start.7
  89.6 1.5 copy-start.9
  89.6 1.5 copy-start.11
  89.6 1.5 copy-start.13
  89.6 1.5 copy-start.15
  91.0 1.4 copy-start.5
  91.0 1.4 copy-start.33
  91.1 1.4 copy-start.35
  91.1 1.3 copy-start.37
  91.1 1.3 copy-start.39
  92.4 1.4 copy-start.3
  92.4 1.4 copy-start.17
  92.4 1.4 copy-start.19
  92.5 1.4 copy-start.21
  92.5 1.4 copy-start.23
  94.4 1.1 copy-start.29
  94.4 1.2 copy-start.31
  95.6 1.0 copy-start.45
  95.6 1.1 copy-start.47
  95.6 1.2 copy-start.49
  (18 other events, 15.4 us)
where the time goes:
time: 155 us; the launch traced here: 154 us
  starting transfers between devices  53.8 us (35%)
  blocking collectives  45.4 us (29%)
  other arithmetic  23.9 us (15%)
  local copies, waits for them, and re-layouts  20.2 us (13%)
  waiting for transfers between devices  6.46 us (4%)
  between operations  4.46 us (3%)
    psum x5, blocking collectives, over_axes(): value = lax.psum(value, axis)  45.4 us
    ppermute x6, starting transfers between devices, padded(): lax.ppermute(lax.slice_in_dim(block, 0, width, axis=dim), axis, backward)  39.7 us
    ppermute x6, starting transfers between devices, padded(): lax.ppermute(lax.slice_in_dim(block, block.shape[dim] - width, None, axis...  14.1 us
    another operation x2, local copies, waits for them, and re-layouts, per_device(): jnp.stack([jnp.sum(vector * vector, axis=(0, 2, 3)) for vector in chebysh...  10.2 us
    reduce_sum x11, other arithmetic, per_device(): jnp.sum(vector * vector, axis=(0, 2, 3))  8.87 us
    sub x10, other arithmetic, per_device(): following = 2.0 * applied - shrink(previous, previous_margin - margin + 1)  5.76 us
    ppermute x6, waiting for transfers between devices, padded(): lax.ppermute(lax.slice_in_dim(block, block.shape[dim] - width, None, axis...  5.16 us
  transfers between devices with their start and end apart: 12, of which 3 were waited for; matrix products, arithmetic and copies ran while one was open for 5% of the time, Pallas kernels for 0%

commit v1 on v0

--- a/solution.py
+++ b/solution.py
@@ -30,7 +30,7 @@
 
 def over_axes(value, axes):
     for axis in axes:
-        value = lax.psum(value, axis)
+        value = jnp.sum(lax.all_gather(value, axis), axis=0)
     return value
 
 

time: 155 us -> 208 us (1.34)
  the two profiles are of different devices: /device:TPU:2 before, /device:TPU:10 now
where the time goes in v1:
time: 208 us; the launch traced here: 207 us
  blocking collectives  90.7 us (44%)
  starting transfers between devices  52.6 us (25%)
  local copies, waits for them, and re-layouts  30.1 us (14%)
  other arithmetic  24.3 us (12%)
  between operations  7.74 us (4%)
    unnamed x5, blocking collectives  47.1 us
    all_gather x5, blocking collectives, over_axes(): value = jnp.sum(lax.all_gather(value, axis), axis=0)  43.7 us
    ppermute x6, starting transfers between devices, padded(): lax.ppermute(lax.slice_in_dim(block, 0, width, axis=dim), axis, backward)  34.1 us
    ppermute x6, starting transfers between devices, padded(): lax.ppermute(lax.slice_in_dim(block, block.shape[dim] - width, None, axis...  18.5 us
    unnamed x126, local copies, waits for them, and re-layouts  11.8 us
    another operation x2, local copies, waits for them, and re-layouts, per_device(): jnp.stack([jnp.sum(vector * vector, axis=(0, 2, 3)) for vector in chebysh...  10.4 us
    reduce_sum x11, other arithmetic, per_device(): jnp.sum(vector * vector, axis=(0, 2, 3))  9.2 us
    sub x10, other arithmetic, per_device(): following = 2.0 * applied - shrink(previous, previous_margin - margin + 1)  5.74 us
  transfers between devices with their start and end apart: 12, of which 2 were waited for; matrix products, arithmetic and copies ran while one was open for 7% of the time, Pallas kernels for 0%

profile of v1, /device:TPU:10, one launch (start us, length us, event | category | flops | bytes accessed | tf_op | source)
XLA Modules:
  0.0 206.7 jit_solution(11170119525599965245)
XLA Ops:
  0.7 1.3 fusion.130
  2.6 0.7 fusion.97
  3.3 1.1 multiply_bitcast_fusion
  4.4 1.9 collective-permute-start.4
  6.4 11.9 %collective-permute-start.5 = (f32[2,1,7,1024]{3,2,1,0:T(8,128)S(1)}, f32[2,1,7,1024]{3,2,1,0:T(8,128)S(1)}, u32[]{:S(2)}, u32[]{:S(2)}) collective-permute-start(f32[2,1,7,1024]{3,2,1,0:T(8,128)S(1)} %get-tuple-element.75), channel_id=1, source_target_pairs={{16,0},{32,16},{48,32},{64,48},{80,64},{96,80},{112,96},{128,112},... | collective-permute-start | bytes 172040 | tf_op jit(solution)/shard_map/ppermute | solution.py:26
  18.9 1.9 collective-permute-start
  20.8 7.3 %collective-permute-start.1 = (f32[3,7,1024]{2,1,0:T(8,128)S(1)}, f32[3,7,1024]{2,1,0:T(8,128)S(1)}, u32[]{:S(2)}, u32[]{:S(2)}) collective-permute-start(f32[3,7,1024]{2,1,0:T(8,128)S(1)} %get-tuple-element.47), channel_id=1, source_target_pairs={{16,0},{32,16},{48,32},{64,48},{80,64},{96,80},{112,96},{128,112},... | collective-permute-start | bytes 258056 | tf_op jit(solution)/shard_map/ppermute | solution.py:26
  29.4 0.7 multiply_reduce_fusion.8
  30.4 3.3 %collective-permute-start.3 = (f32[3,46,7]{2,1,0:T(8,128)S(1)}, f32[3,46,7]{2,1,0:T(8,128)S(1)}, u32[]{:S(2)}, u32[]{:S(2)}) collective-permute-start(f32[3,46,7]{2,1,0:T(8,128)S(1)} %get-tuple-element.34), channel_id=1, source_target_pairs={{1,0},{2,1},{3,2},{4,3},{5,4},{6,5},{7,6},{8,7},{9,8},{10,9},{11,1... | collective-permute-start | bytes 11600 | tf_op jit(solution)/shard_map/ppermute | solution.py:26
  33.8 3.4 %collective-permute-start.2 = (f32[3,46,7]{2,1,0:T(8,128)S(1)}, f32[3,46,7]{2,1,0:T(8,128)S(1)}, u32[]{:S(2)}, u32[]{:S(2)}) collective-permute-start(f32[3,46,7]{2,1,0:T(8,128)S(1)} %get-tuple-element.35), channel_id=1, source_target_pairs={{0,1},{1,2},{2,3},{3,4},{4,5},{5,6},{6,7},{7,8},{8,9},{9,10},{10,1... | collective-permute-start | bytes 11600 | tf_op jit(solution)/shard_map/ppermute | solution.py:23
  37.3 2.4 %collective-permute-start.7 = (f32[2,1,46,7]{3,2,1,0:T(8,128)S(1)}, f32[2,1,46,7]{3,2,1,0:T(8,128)S(1)}, u32[]{:S(2)}, u32[]{:S(2)}) collective-permute-start(f32[2,1,46,7]{3,2,1,0:T(8,128)S(1)} %get-tuple-element.48), channel_id=1, source_target_pairs={{1,0},{2,1},{3,2},{4,3},{5,4},{6,5},{7,6},{8,7},{9,8},{10,9},{11,1... | collective-permute-start | bytes 7736 | tf_op jit(solution)/shard_map/ppermute | solution.py:26
  39.7 4.3 %collective-permute-start.6 = (f32[2,1,46,7]{3,2,1,0:T(8,128)S(1)}, f32[2,1,46,7]{3,2,1,0:T(8,128)S(1)}, u32[]{:S(2)}, u32[]{:S(2)}) collective-permute-start(f32[2,1,46,7]{3,2,1,0:T(8,128)S(1)} %get-tuple-element.49), channel_id=1, source_target_pairs={{0,1},{1,2},{2,3},{3,4},{4,5},{5,6},{6,7},{7,8},{8,9},{9,10},{10,1... | collective-permute-start | bytes 7736 | tf_op jit(solution)/shard_map/ppermute | solution.py:23
  44.1 1.3 dynamic-slice.4
  45.4 1.3 dynamic-slice.3
  48.0 1.3 dynamic-slice.2
  49.9 1.3 dynamic-slice.1
  51.8 1.3 dynamic-slice
  56.7 0.7 fusion.65
  58.7 0.8 fusion.64
  65.2 1.1 multiply_reduce_fusion.4
  66.4 0.8 multiply_reduce_fusion.10
  67.2 1.9 collective-permute-start.8
  69.1 7.3 %collective-permute-start.9 = (f32[2,1,7,1024]{3,2,1,0:T(8,128)S(1)}, f32[2,1,7,1024]{3,2,1,0:T(8,128)S(1)}, u32[]{:S(2)}, u32[]{:S(2)}) collective-permute-start(f32[2,1,7,1024]{3,2,1,0:T(8,128)S(1)} %get-tuple-element.71), channel_id=1, source_target_pairs={{16,0},{32,16},{48,32},{64,48},{80,64},{96,80},{112,96},{128,112},... | collective-permute-start | bytes 172040 | tf_op jit(solution)/shard_map/ppermute | solution.py:26
  76.4 0.7 fusion.63
  77.1 1.1 collective-permute-done.9
  78.4 1.9 collective-permute-start.11
  80.3 5.0 %collective-permute-start.10 = (f32[2,1,46,7]{3,2,1,0:T(8,128)S(1)}, f32[2,1,46,7]{3,2,1,0:T(8,128)S(1)}, u32[]{:S(2)}, u32[]{:S(2)}) collective-permute-start(f32[2,1,46,7]{3,2,1,0:T(8,128)S(1)} %get-tuple-element.45), channel_id=1, source_target_pairs={{0,1},{1,2},{2,3},{3,4},{4,5},{5,6},{6,7},{7,8},{8,9},{9,10},{10,1... | collective-permute-start | bytes 7736 | tf_op jit(solution)/shard_map/ppermute | solution.py:23
  85.3 0.8 multiply_reduce_fusion.7
  86.1 5.1 %stack.186 = f32[8,1]{0,1:T(1,128)S(1)} concatenate(f32[1,1]{0,1:T(1,128)} %bitcast.40, f32[1,1]{0,1:T(1,128)} %bitcast.41, f32[1,1]{0,1:T(1,128)} %bitcast.42, f32[1,1]{0,1:T(1,128)} %bitcast.43, f32[1,1]{0,1:T(1,128)} %bitcast.44, f32[1,1]{0,1:T(1,128)} %bitcast.45, f32[1,1]{0,1:T(1,128)} %bitcast.46, f32[1,1]{0,1:T(1,128)} %bitcast.47), dimensions={0} | concatenate | bytes 64 | tf_op jit(solution)/shard_map/stack | solution.py:128
  92.1 0.8 fusion.62
  99.6 1.1 multiply_reduce_fusion
  101.1 0.9 multiply_reduce_fusion.9
  102.0 1.4 fusion.102
  103.3 14.8 %all-reduce = f32[16]{0:T(128)S(1)} all-reduce(f32[16]{0:T(128)S(1)} %fusion.102), channel_id=2, replica_groups=mesh['gx_0'=8,'gx_1'=2,'gx_2'=2,'gy_0'=8,'gy_1'=2] {'gx_0'}, use_global_device_ids=true, to_apply=%add | all-reduce | flops 16 | bytes 128
  118.5 0.8 fusion.61
  119.3 6.4 %all-reduce.1 = f32[4]{0:T(128)S(1)} all-reduce(f32[4]{0:T(128)S(1)} %dynamic-update-slice.1), channel_id=3, replica_groups=mesh['gx_0'=8,'gx_1'=2,'gx_2'=2,'gy_0'=8,'gy_1'=2] {'gx_1'}, use_global_device_ids=true, to_apply=%add.1 | all-reduce | flops 4 | bytes 32
  126.1 0.8 fusion.60
  126.9 2.4 %all-reduce.2 = f32[4]{0:T(128)S(1)} all-reduce(f32[4]{0:T(128)S(1)} %dynamic-update-slice.2), channel_id=4, replica_groups=mesh['gx_0'=8,'gx_1'=2,'gx_2'=2,'gy_0'=8,'gy_1'=2] {'gx_2'}, use_global_device_ids=true, to_apply=%add.2 | all-reduce | flops 4 | bytes 32
  129.7 18.5 %all-reduce.3 = f32[16]{0:T(128)S(1)} all-reduce(f32[16]{0:T(128)S(1)} %dynamic-update-slice.3), channel_id=5, replica_groups=mesh['gx_0'=8,'gx_1'=2,'gx_2'=2,'gy_0'=8,'gy_1'=2] {'gy_0'}, use_global_device_ids=true, to_apply=%add.3 | all-reduce | flops 16 | bytes 128
  148.5 0.8 multiply_reduce_fusion.3
  149.3 4.9 %all-reduce.4 = f32[4]{0:T(128)S(1)} all-reduce(f32[4]{0:T(128)S(1)} %dynamic-update-slice.4), channel_id=6, replica_groups=mesh['gx_0'=8,'gx_1'=2,'gx_2'=2,'gy_0'=8,'gy_1'=2] {'gy_1'}, use_global_device_ids=true, to_apply=%add.4 | all-reduce | flops 4 | bytes 32
  156.3 0.7 slice_bitcast_fusion.21
  157.1 5.3 %stack.195 = f32[8,1]{0,1:T(1,128)S(1)} concatenate(f32[1,1]{0,1:T(1,128)} %bitcast.29, f32[1,1]{0,1:T(1,128)} %bitcast.49, f32[1,1]{0,1:T(1,128)} %bitcast.50, f32[1,1]{0,1:T(1,128)} %bitcast.51, f32[1,1]{0,1:T(1,128)} %bitcast.52, f32[1,1]{0,1:T(1,128)} %bitcast.53, f32[1,1]{0,1:T(1,128)} %bitcast.54, f32[1,1]{0,1:T(1,128)} %bitcast.55), dimensions={0} | concatenate | bytes 64 | tf_op jit(solution)/shard_map/stack | solution.py:128
  162.3 15.4 %all-gather.5 = f32[16,8,1]{1,2,0:T(1,128)S(1)} all-gather(f32[2,8,1]{1,2,0:T(1,128)S(1)} %pad_maximum_fusion.7), channel_id=7, replica_groups=mesh['gx_0'=8,'gx_1'=2,'gx_2'=2,'gy_0'=8,'gy_1'=2] {'gx_0'}, dimensions={0}, use_global_device_ids=true | all-gather | bytes 576 | tf_op jit(solution)/shard_map/all_gather | solution.py:33
  177.7 5.7 %all-gather.10 = f32[2,2,8]{2,1,0:T(2,128)S(1)} all-gather(f32[1,2,8]{2,1,0:T(2,128)S(1)} %bitcast.107), channel_id=8, replica_groups=mesh['gx_0'=8,'gx_1'=2,'gx_2'=2,'gy_0'=8,'gy_1'=2] {'gx_1'}, dimensions={0}, use_global_device_ids=true | all-gather | bytes 192 | tf_op jit(solution)/shard_map/all_gather | solution.py:33
  183.5 1.8 all-gather.11
  185.3 16.5 %all-gather.12 = f32[8,2,8]{2,1,0:T(2,128)S(1)} all-gather(f32[1,2,8]{2,1,0:T(2,128)S(1)} %bitcast.109), channel_id=10, replica_groups=mesh['gx_0'=8,'gx_1'=2,'gx_2'=2,'gy_0'=8,'gy_1'=2] {'gy_0'}, dimensions={0}, use_global_device_ids=true | all-gather | bytes 576 | tf_op jit(solution)/shard_map/all_gather | solution.py:33
  201.8 4.2 %all-gather.13 = f32[2,2,8]{2,1,0:T(2,128)S(1)} all-gather(f32[1,2,8]{2,1,0:T(2,128)S(1)} %bitcast.110), channel_id=11, replica_groups=mesh['gx_0'=8,'gx_1'=2,'gx_2'=2,'gy_0'=8,'gy_1'=2] {'gy_1'}, dimensions={0}, use_global_device_ids=true | all-gather | bytes 192 | tf_op jit(solution)/shard_map/all_gather | solution.py:33
  (211 shorter events, 21.7 us)
Async XLA Ops:
  0.6 17.7 %copy-start.55 = (f32[16]{0:T(128)S(1)}, f32[16]{0:T(128)}, u32[]{:S(2)}) copy-start(f32[16]{0:T(128)} %param.13) | copy-start | bytes 196
  0.6 17.7 %copy-start.54 = (s32[32,1024]{1,0:T(8,128)S(1)}, s32[32,1024]{1,0:T(8,128)}, u32[]{:S(2)}) copy-start(s32[32,1024]{1,0:T(8,128)} %param.12) | copy-start | bytes 393220
  0.7 17.7 %copy-start.53 = (s32[32,1024]{1,0:T(8,128)S(1)}, s32[32,1024]{1,0:T(8,128)}, u32[]{:S(2)}) copy-start(s32[32,1024]{1,0:T(8,128)} %param.11) | copy-start | bytes 393220
  3.3 15.5 %copy-start.52 = (f32[32,1024]{1,0:T(8,128)S(1)}, f32[32,1024]{1,0:T(8,128)}, u32[]{:S(2)}) copy-start(f32[32,1024]{1,0:T(8,128)} %param.10) | copy-start | bytes 393220
  4.4 25.7 %collective-permute-start.4 = (f32[2,1,7,1024]{3,2,1,0:T(8,128)S(1)}, f32[2,1,7,1024]{3,2,1,0:T(8,128)S(1)}, u32[]{:S(2)}, u32[]{:S(2)}) collective-permute-start(f32[2,1,7,1024]{3,2,1,0:T(8,128)S(1)} %get-tuple-element.74), channel_id=1, source_target_pairs={{0,16},{16,32},{32,48},{48,64},{64,80},{80,96},{96,112},{112,128},... | collective-permute-start | bytes 172040 | tf_op jit(solution)/shard_map/ppermute | solution.py:23
  6.4 23.8 %collective-permute-start.5 = (f32[2,1,7,1024]{3,2,1,0:T(8,128)S(1)}, f32[2,1,7,1024]{3,2,1,0:T(8,128)S(1)}, u32[]{:S(2)}, u32[]{:S(2)}) collective-permute-start(f32[2,1,7,1024]{3,2,1,0:T(8,128)S(1)} %get-tuple-element.75), channel_id=1, source_target_pairs={{16,0},{32,16},{48,32},{64,48},{80,64},{96,80},{112,96},{128,112},... | collective-permute-start | bytes 172040 | tf_op jit(solution)/shard_map/ppermute | solution.py:26
  18.9 11.3 %collective-permute-start = (f32[3,7,1024]{2,1,0:T(8,128)S(1)}, f32[3,7,1024]{2,1,0:T(8,128)S(1)}, u32[]{:S(2)}, u32[]{:S(2)}) collective-permute-start(f32[3,7,1024]{2,1,0:T(8,128)S(1)} %get-tuple-element.46), channel_id=1, source_target_pairs={{0,16},{16,32},{32,48},{48,64},{64,80},{80,96},{96,112},{112,128},... | collective-permute-start | bytes 258056 | tf_op jit(solution)/shard_map/ppermute | solution.py:23
  20.8 9.5 %collective-permute-start.1 = (f32[3,7,1024]{2,1,0:T(8,128)S(1)}, f32[3,7,1024]{2,1,0:T(8,128)S(1)}, u32[]{:S(2)}, u32[]{:S(2)}) collective-permute-start(f32[3,7,1024]{2,1,0:T(8,128)S(1)} %get-tuple-element.47), channel_id=1, source_target_pairs={{16,0},{32,16},{48,32},{64,48},{80,64},{96,80},{112,96},{128,112},... | collective-permute-start | bytes 258056 | tf_op jit(solution)/shard_map/ppermute | solution.py:26
  30.4 23.5 %collective-permute-start.3 = (f32[3,46,7]{2,1,0:T(8,128)S(1)}, f32[3,46,7]{2,1,0:T(8,128)S(1)}, u32[]{:S(2)}, u32[]{:S(2)}) collective-permute-start(f32[3,46,7]{2,1,0:T(8,128)S(1)} %get-tuple-element.34), channel_id=1, source_target_pairs={{1,0},{2,1},{3,2},{4,3},{5,4},{6,5},{7,6},{8,7},{9,8},{10,9},{11,1... | collective-permute-start | bytes 11600 | tf_op jit(solution)/shard_map/ppermute | solution.py:26
  33.8 20.2 %collective-permute-start.2 = (f32[3,46,7]{2,1,0:T(8,128)S(1)}, f32[3,46,7]{2,1,0:T(8,128)S(1)}, u32[]{:S(2)}, u32[]{:S(2)}) collective-permute-start(f32[3,46,7]{2,1,0:T(8,128)S(1)} %get-tuple-element.35), channel_id=1, source_target_pairs={{0,1},{1,2},{2,3},{3,4},{4,5},{5,6},{6,7},{7,8},{8,9},{9,10},{10,1... | collective-permute-start | bytes 11600 | tf_op jit(solution)/shard_map/ppermute | solution.py:23
  37.3 16.5 %collective-permute-start.7 = (f32[2,1,46,7]{3,2,1,0:T(8,128)S(1)}, f32[2,1,46,7]{3,2,1,0:T(8,128)S(1)}, u32[]{:S(2)}, u32[]{:S(2)}) collective-permute-start(f32[2,1,46,7]{3,2,1,0:T(8,128)S(1)} %get-tuple-element.48), channel_id=1, source_target_pairs={{1,0},{2,1},{3,2},{4,3},{5,4},{6,5},{7,6},{8,7},{9,8},{10,9},{11,1... | collective-permute-start | bytes 7736 | tf_op jit(solution)/shard_map/ppermute | solution.py:26
  39.7 14.0 %collective-permute-start.6 = (f32[2,1,46,7]{3,2,1,0:T(8,128)S(1)}, f32[2,1,46,7]{3,2,1,0:T(8,128)S(1)}, u32[]{:S(2)}, u32[]{:S(2)}) collective-permute-start(f32[2,1,46,7]{3,2,1,0:T(8,128)S(1)} %get-tuple-element.49), channel_id=1, source_target_pairs={{0,1},{1,2},{2,3},{3,4},{4,5},{5,6},{6,7},{7,8},{8,9},{9,10},{10,1... | collective-permute-start | bytes 7736 | tf_op jit(solution)/shard_map/ppermute | solution.py:23
  59.7 4.3 %copy-start.4 = (f32[34,1026]{1,0:T(8,128)}, f32[34,1026]{1,0:T(8,128)S(1)}, u32[]{:S(2)}) copy-start(f32[34,1026]{1,0:T(8,128)S(1)} %slice.964) | copy-start | bytes 418612
  59.9 2.3 %copy-start.8 = (f32[38,1030]{1,0:T(8,128)}, f32[38,1030]{1,0:T(8,128)S(1)}, u32[]{:S(2)}) copy-start(f32[38,1030]{1,0:T(8,128)S(1)} %slice.934) | copy-start | bytes 469684
  60.0 3.0 %copy-start.6 = (f32[36,1028]{1,0:T(8,128)}, f32[36,1028]{1,0:T(8,128)S(1)}, u32[]{:S(2)}) copy-start(f32[36,1028]{1,0:T(8,128)S(1)} %slice.948) | copy-start | bytes 444100
  60.5 1.0 copy-start.20
  60.5 1.0 copy-start.22
  61.9 1.1 copy-start.10
  61.9 1.1 copy-start.12
  61.9 1.1 copy-start.14
  61.9 1.1 copy-start.16
  65.2 1.1 copy-start.44
  65.2 1.1 copy-start.46
  65.2 1.1 copy-start.48
  65.2 1.1 copy-start.50
  67.2 9.9 %collective-permute-start.8 = (f32[2,1,7,1024]{3,2,1,0:T(8,128)S(1)}, f32[2,1,7,1024]{3,2,1,0:T(8,128)S(1)}, u32[]{:S(2)}, u32[]{:S(2)}) collective-permute-start(f32[2,1,7,1024]{3,2,1,0:T(8,128)S(1)} %get-tuple-element.70), channel_id=1, source_target_pairs={{0,16},{16,32},{32,48},{48,64},{64,80},{80,96},{96,112},{112,128},... | collective-permute-start | bytes 172040 | tf_op jit(solution)/shard_map/ppermute | solution.py:23
  69.1 9.1 %collective-permute-start.9 = (f32[2,1,7,1024]{3,2,1,0:T(8,128)S(1)}, f32[2,1,7,1024]{3,2,1,0:T(8,128)S(1)}, u32[]{:S(2)}, u32[]{:S(2)}) collective-permute-start(f32[2,1,7,1024]{3,2,1,0:T(8,128)S(1)} %get-tuple-element.71), channel_id=1, source_target_pairs={{16,0},{32,16},{48,32},{64,48},{80,64},{96,80},{112,96},{128,112},... | collective-permute-start | bytes 172040 | tf_op jit(solution)/shard_map/ppermute | solution.py:26
  78.4 12.9 %collective-permute-start.11 = (f32[2,1,46,7]{3,2,1,0:T(8,128)S(1)}, f32[2,1,46,7]{3,2,1,0:T(8,128)S(1)}, u32[]{:S(2)}, u32[]{:S(2)}) collective-permute-start(f32[2,1,46,7]{3,2,1,0:T(8,128)S(1)} %get-tuple-element.44), channel_id=1, source_target_pairs={{1,0},{2,1},{3,2},{4,3},{5,4},{6,5},{7,6},{8,7},{9,8},{10,9},{11,1... | collective-permute-start | bytes 7736 | tf_op jit(solution)/shard_map/ppermute | solution.py:26
  80.3 11.0 %collective-permute-start.10 = (f32[2,1,46,7]{3,2,1,0:T(8,128)S(1)}, f32[2,1,46,7]{3,2,1,0:T(8,128)S(1)}, u32[]{:S(2)}, u32[]{:S(2)}) collective-permute-start(f32[2,1,46,7]{3,2,1,0:T(8,128)S(1)} %get-tuple-element.45), channel_id=1, source_target_pairs={{0,1},{1,2},{2,3},{3,4},{4,5},{5,6},{6,7},{7,8},{8,9},{9,10},{10,1... | collective-permute-start | bytes 7736 | tf_op jit(solution)/shard_map/ppermute | solution.py:23
  91.6 1.4 copy-start.1
  91.6 1.4 copy-start.3
  92.9 1.0 copy-start.21
  92.9 1.1 copy-start.23
  92.9 1.2 copy-start.25
  93.0 1.2 copy-start.27
  94.8 1.1 copy-start.31
  94.8 1.2 copy-start.33
  94.8 1.2 copy-start.35
  96.0 1.0 copy-start.11
  96.0 1.1 copy-start.13
  96.0 1.2 copy-start.15
  96.0 1.2 copy-start.17
  97.3 1.0 copy-start.37
  97.3 1.1 copy-start.39
  97.3 1.2 copy-start.41
  97.3 1.2 copy-start.43
  98.5 1.0 copy-start.49
  98.5 1.1 copy-start.51
  (20 other events, 16.8 us)
